TPU v7x, 32 devices: a whole 2x2x4 slice. The times are simulated.
32 devices in a mesh: tilt: 2 (over y), row: 8 (over z, x), col: 2 (over core).
Axes of the slice: x: 2, y: 2, z: 4, core: 2. Of those that a mesh axis runs over, the one named last changes fastest.
Arguments:
- object_field: float32 [2, 2048, 256], P(None, ('tilt', 'row'), 'col'), parts along dimension 1, may hold values from -4.2 to 4.2
- probe: float32 [8, 2, 128, 128], P('tilt'), parts along dimension 0, may hold values from -2.1 to 2.1
- patterns: float32 [16, 2, 2, 128, 128], P(('tilt', 'row'), 'col'), parts along dimension 0, may hold values from 0.1 to 3
- offsets: int32 [16, 2, 2, 2], P(('tilt', 'row'), 'col'), parts along dimension 0, may hold values from 0 to 256
- counts: int32 [16, 2], P(('tilt', 'row'), 'col'), parts along dimension 0, may hold values from 1 to 2, as said below
Outputs:
- object_out: float32 [2, 2048, 256], P(None, ('tilt', 'row'), 'col'), parts along dimension 1
- probe_out: float32 [8, 2, 128, 128], P('tilt'), parts along dimension 0
There are 2 independent parts, one for each index of `tilt`. A program takes and returns all parts, laid end to end along the dimension named above; each array names one. Nothing has to cross between parts.
Inputs may be any that keep to these rules, and one draw needn't show every extreme that they name: Only the first counts[r, c] slots of a tile are live; some tile has all 2 live. `offsets`: A window lies inside its tile's frame of 384 pixels a side.
All inputs are finite; a program needn't handle non-finite values.
Results may differ from a plain program's by a relative error of at most 0.0003.
Values sent between devices are 32-bit elements; how exact they have to be, the bound alone decides.
A program may use at most 64 MiB of HBM per device.

v0:
```python
import jax
import jax.numpy as jnp
from jax import lax
from jax.sharding import PartitionSpec as P

H = 128
object_rate = 1.0
probe_rate = 1.0
epsilon = 1e-06


def with_halo(block, sides, width):
    for axis, dim in sides:
        count = lax.axis_size(axis)
        forward = [(i, i + 1) for i in range(count - 1)]
        backward = [(target, source) for source, target in forward]
        low = lax.ppermute(
            lax.slice_in_dim(block, block.shape[dim] - width, None, axis=dim), axis, forward
        )
        high = lax.ppermute(lax.slice_in_dim(block, 0, width, axis=dim), axis, backward)
        block = jnp.concatenate([low, block, high], axis=dim)
    return block


def as_index(value):
    return jnp.asarray(value).astype(jnp.int32)


def dft_tables(length):
    counter = jnp.arange(length, dtype=jnp.int32)
    product = counter[:, None] * counter[None, :] % length
    angle = -2.0 * jnp.pi / length * product.astype(jnp.float32)
    norm = 1.0 / jnp.sqrt(jnp.float32(length))
    return (jnp.cos(angle) * norm, jnp.sin(angle) * norm)


def left_product(cos_table, sin_table, real_part, imag_part):
    hp = lax.Precision.HIGHEST
    real_out = jnp.einsum("ab,kbc->kac", cos_table, real_part, precision=hp) - jnp.einsum(
        "ab,kbc->kac", sin_table, imag_part, precision=hp
    )
    imag_out = jnp.einsum("ab,kbc->kac", cos_table, imag_part, precision=hp) + jnp.einsum(
        "ab,kbc->kac", sin_table, real_part, precision=hp
    )
    return (real_out, imag_out)


def right_product(real_part, imag_part, cos_table, sin_table):
    hp = lax.Precision.HIGHEST
    real_out = jnp.einsum("kab,bc->kac", real_part, cos_table, precision=hp) - jnp.einsum(
        "kab,bc->kac", imag_part, sin_table, precision=hp
    )
    imag_out = jnp.einsum("kab,bc->kac", real_part, sin_table, precision=hp) + jnp.einsum(
        "kab,bc->kac", imag_part, cos_table, precision=hp
    )
    return (real_out, imag_out)


def transform(real_part, imag_part, cos_table, sin_table):
    middle_re, middle_im = left_product(cos_table, sin_table, real_part, imag_part)
    return right_product(middle_re, middle_im, cos_table, sin_table)


def slot_terms(window, probe, pattern, cos_table, sin_table):
    window_re, window_im = (window[0], window[1])
    probe_re, probe_im = (probe[:, 0], probe[:, 1])
    exit_re = probe_re * window_re - probe_im * window_im
    exit_im = probe_re * window_im + probe_im * window_re
    far_re, far_im = transform(exit_re, exit_im, cos_table, sin_table)
    intensity = jnp.sum(far_re * far_re + far_im * far_im, axis=0)
    misfit = intensity - pattern
    back_re, back_im = transform(misfit * far_re, misfit * far_im, cos_table, -sin_table)
    grad_re = jnp.sum(probe_re * back_re + probe_im * back_im, axis=0)
    grad_im = jnp.sum(probe_re * back_im - probe_im * back_re, axis=0)
    term_re = window_re * back_re + window_im * back_im
    term_im = window_re * back_im - window_im * back_re
    return (jnp.stack([grad_re, grad_im]), jnp.stack([term_re, term_im], axis=1))


def body(object_field, probe, patterns, offsets, counts):
    width = probe.shape[-1]
    block = object_field.shape[1]
    slot_total = patterns.shape[2]
    cos_table, sin_table = dft_tables(width)
    tile_total = lax.axis_size("row") * lax.axis_size("col")
    live_count = counts[0, 0]
    frame = with_halo(object_field, (("row", 1), ("col", 2)), H)

    def slot_step(slot_index, inner):
        local_grad, probe_acc = inner
        slot_index = as_index(slot_index)
        corner_y = as_index(offsets[0, 0, slot_index, 0])
        corner_x = as_index(offsets[0, 0, slot_index, 1])
        window = lax.dynamic_slice(frame, (as_index(0), corner_y, corner_x), (2, width, width))
        window_grad, probe_term = slot_terms(
            window, probe, patterns[0, 0, slot_index], cos_table, sin_table
        )
        live = (slot_index < live_count).astype(jnp.float32)
        region = (
            lax.dynamic_slice(local_grad, (as_index(0), corner_y, corner_x), (2, width, width))
            + live * window_grad
        )
        local_grad = lax.dynamic_update_slice(local_grad, region, (as_index(0), corner_y, corner_x))
        return (local_grad, probe_acc + live * probe_term)

    start_carry = (jnp.zeros_like(frame), jnp.zeros_like(probe))
    gradient, probe_grad = lax.fori_loop(0, slot_total, slot_step, start_carry)
    upper_strip = gradient[:, :H, :]
    lower_strip = gradient[:, H + block :, :]
    middle = gradient[:, H : H + block, :]
    row_edges = jnp.concatenate([upper_strip, lower_strip], axis=1)
    row_grown = with_halo(row_edges, (("row", 1),), H)
    from_above = row_grown[:, :H, :]
    from_below = row_grown[:, 3 * H :, :]
    middle = middle.at[:, :H, :].add(from_above).at[:, block - H :, :].add(from_below)
    left_strip = middle[:, :, :H]
    right_strip = middle[:, :, H + block :]
    object_grad = middle[:, :, H : H + block]
    col_edges = jnp.concatenate([left_strip, right_strip], axis=2)
    col_grown = with_halo(col_edges, (("col", 2),), H)
    from_left = col_grown[:, :, :H]
    from_right = col_grown[:, :, 3 * H :]
    object_grad = object_grad.at[:, :, :H].add(from_left).at[:, :, block - H :].add(from_right)
    weight = (
        jnp.max(jnp.sum(probe[:, 0] * probe[:, 0] + probe[:, 1] * probe[:, 1], axis=0)) + epsilon
    )
    object_field = object_field - object_rate * object_grad / weight
    summed = lax.psum(probe_grad, ("row", "col"))
    probe = probe - probe_rate * summed / tile_total
    return (object_field, probe)


def solution(mesh):
    placed = (
        P(None, ("tilt", "row"), "col"),
        P("tilt", None, None, None),
        P(("tilt", "row"), "col", None, None, None),
        P(("tilt", "row"), "col", None, None),
        P(("tilt", "row"), "col"),
    )
    return jax.shard_map(
        body,
        mesh=mesh,
        in_specs=placed,
        out_specs=(P(None, ("tilt", "row"), "col"), P("tilt", None, None, None)),
        check_vma=False,
    )
```

profile of v0, /device:TPU:0, one launch (start us, length us, event | category | flops | bytes accessed | tf_op | source)
XLA Modules:
  0.0 179.6 jit_solution(4061278362378386647)
XLA Ops:
  7.2 4.9 %collective-permute-start = (f32[2,128,128]{2,1,0:T(8,128)}, f32[2,128,128]{2,1,0:T(8,128)S(1)}, u32[]{:S(2)}, u32[]{:S(2)}) collective-permute-start(f32[2,128,128]{2,1,0:T(8,128)} %param.23), channel_id=1, source_target_pairs={{0,2},{2,4},{4,6},{6,8},{8,10},{10,12},{12,14},{1,3},{3,5},{5,7},{... | collective-permute-start | bytes 393224 | tf_op jit(solution)/shard_map/ppermute | solution.py:17
  12.1 1.3 collective-permute-start.1
  13.4 1.7 collective-permute-done
  15.2 0.9 constant_dynamic-update-slice_fusion.1
  16.1 3.1 %collective-permute-done.1 = f32[2,128,128]{2,1,0:T(8,128)S(1)} collective-permute-done((f32[2,128,128]{2,1,0:T(8,128)}, f32[2,128,128]{2,1,0:T(8,128)S(1)}, u32[]{:S(2)}, u32[]{:S(2)}) %collective-permute-start.1) | collective-permute-done | bytes 131104 | tf_op jit(solution)/shard_map/ppermute | solution.py:20
  19.2 1.3 collective-permute-start.2
  20.5 1.3 collective-permute-start.3
  21.8 1.1 copy.41
  22.9 1.2 collective-permute-done.3
  24.1 1.1 pad_maximum_fusion
  25.3 0.8 copy-done.1
  26.1 42.0 %while.26 = (s32[]{:T(128)}, f32[2,384,384]{2,1,0:T(8,128)S(1)}, f32[4,2,128,128]{3,2,0,1:T(8,128)S(1)}, s32[1,1,2,2]{3,2,1,0:T(2,128)S(1)}, s32[]{:T(128)}, /*i...) while((s32[]{:T(128)}, f32[2,384,384]{2,1,0:T(8,128)S(1)}, ...), condition=%wide.region_4.5_spmd.clone.clone, body=%wide.region_0.4_spmd.clone.clone.sunk | while | flops 1617952768 | bytes 16646421 | solution.py:107
  30.7 1.1 dynamic-slice_bitcast_fusion.3
  44.8 2.2 %dynamic_update_slice.11 = f32[2,384,384]{2,1,0:T(8,128)S(1)} dynamic-update-slice(f32[2,384,384]{2,1,0:T(8,128)S(1)} %get-tuple-element.543, f32[2,128,128]{2,1,0:T(8,128)S(1)} %fusion.247, s32[]{:T(128)} %constant.191.clone.1..sunk, s32[]{:T(128)S(6)} %select_n.177, s32[]{:T(128)S(6)} %select_n.178) | dynamic-update-slice | bytes 262148 | tf_op jit(solution)/shard_map/while/body/eval_jaxpr/dynamic_update_slice | solution.py:103
  51.6 1.1 dynamic-slice_bitcast_fusion.3
  65.6 2.5 %dynamic_update_slice.11 = f32[2,384,384]{2,1,0:T(8,128)S(1)} dynamic-update-slice(f32[2,384,384]{2,1,0:T(8,128)S(1)} %get-tuple-element.543, f32[2,128,128]{2,1,0:T(8,128)S(1)} %fusion.247, s32[]{:T(128)} %constant.191.clone.1..sunk, s32[]{:T(128)S(6)} %select_n.177, s32[]{:T(128)S(6)} %select_n.178) | dynamic-update-slice | bytes 262148 | tf_op jit(solution)/shard_map/while/body/eval_jaxpr/dynamic_update_slice | solution.py:103
  69.0 4.5 %collective-permute-start.4 = (f32[2,128,384]{2,1,0:T(8,128)}, f32[2,128,384]{2,1,0:T(8,128)S(1)}, u32[]{:S(2)}, u32[]{:S(2)}) collective-permute-start(f32[2,128,384]{2,1,0:T(8,128)} %get-tuple-element.457), channel_id=1, source_target_pairs={{0,2},{2,4},{4,6},{6,8},{8,10},{10,12},{12,14},{1,3},{3,5},{5,7},{... | collective-permute-start | bytes 1179656 | tf_op jit(solution)/shard_map/ppermute | solution.py:17
  73.5 1.3 collective-permute-start.5
  76.1 0.8 copy.42
  77.0 14.1 %collective-permute-done.4 = f32[2,128,384]{2,1,0:T(8,128)S(1)} collective-permute-done((f32[2,128,384]{2,1,0:T(8,128)}, f32[2,128,384]{2,1,0:T(8,128)S(1)}, u32[]{:S(2)}, u32[]{:S(2)}) %collective-permute-start.4) | collective-permute-done | bytes 393248 | tf_op jit(solution)/shard_map/ppermute | solution.py:17
  91.1 1.4 collective-permute-start.6
  92.6 1.3 collective-permute-start.7
  93.9 76.3 %all-reduce.2.cloned.1.call-done = f32[4,2,128,128]{3,2,1,0:T(8,128)} async-done(((f32[4,2,128,128]{3,2,1,0:T(8,128)}), f32[4,2,128,128]{3,2,1,0:T(8,128)}) %all-reduce.2.cloned.1.call-update) | async-done | bytes 524304 | tf_op jit(solution)/shard_map/psum | solution.py:128
  170.2 1.9 %multiply_subtract_fusion = f32[4,2,128,128]{3,2,1,0:T(8,128)} fusion(f32[4,2,128,128]{3,2,1,0:T(8,128)S(1)} %copy-done, f32[4,2,128,128]{3,2,1,0:T(8,128)} %all-reduce.2.cloned.1.call-done), kind=kLoop, calls=%fused_computation.169 | loop fusion | flops 262144 | bytes 1572864 | tf_op jit(solution)/shard_map/sub | solution.py:129
  (63 shorter events, 28.0 us)
Async XLA Ops:
  7.2 163.0 %all-reduce.2.cloned.1.call-start = ((), (), s32[]{:S(2)}) async-start(), calls=%async_computation | async-start | bytes 1048576 | tf_op jit(solution)/shard_map/psum | solution.py:128
  7.2 7.9 %collective-permute-start = (f32[2,128,128]{2,1,0:T(8,128)}, f32[2,128,128]{2,1,0:T(8,128)S(1)}, u32[]{:S(2)}, u32[]{:S(2)}) collective-permute-start(f32[2,128,128]{2,1,0:T(8,128)} %param.23), channel_id=1, source_target_pairs={{0,2},{2,4},{4,6},{6,8},{8,10},{10,12},{12,14},{1,3},{3,5},{5,7},{... | collective-permute-start | bytes 393224 | tf_op jit(solution)/shard_map/ppermute | solution.py:17
  12.1 7.1 %collective-permute-start.1 = (f32[2,128,128]{2,1,0:T(8,128)}, f32[2,128,128]{2,1,0:T(8,128)S(1)}, u32[]{:S(2)}, u32[]{:S(2)}) collective-permute-start(f32[2,128,128]{2,1,0:T(8,128)} %param.23), channel_id=1, source_target_pairs={{2,0},{4,2},{6,4},{8,6},{10,8},{12,10},{14,12},{3,1},{5,3},{7,5},{... | collective-permute-start | bytes 393224 | tf_op jit(solution)/shard_map/ppermute | solution.py:20
  19.2 3.7 %collective-permute-start.2 = (f32[2,384,128]{2,1,0:T(8,128)S(1)}, f32[2,384,128]{2,1,0:T(8,128)S(1)}, u32[]{:S(2)}, u32[]{:S(2)}) collective-permute-start(f32[2,384,128]{2,1,0:T(8,128)S(1)} %constant_dynamic-update-slice_fusion), channel_id=1, source_target_pairs={{0,1},{2,3},{4,5},{6,7},{8,9},{10,11},{12,13},{14,15},{16,17},{18,... | collective-permute-start | bytes 1179656 | tf_op jit(solution)/shard_map/ppermute | solution.py:17
  20.5 3.6 %collective-permute-start.3 = (f32[2,384,128]{2,1,0:T(8,128)S(1)}, f32[2,384,128]{2,1,0:T(8,128)S(1)}, u32[]{:S(2)}, u32[]{:S(2)}) collective-permute-start(f32[2,384,128]{2,1,0:T(8,128)S(1)} %constant_dynamic-update-slice_fusion), channel_id=1, source_target_pairs={{1,0},{3,2},{5,4},{7,6},{9,8},{11,10},{13,12},{15,14},{17,16},{19,... | collective-permute-start | bytes 1179656 | tf_op jit(solution)/shard_map/ppermute | solution.py:20
  25.2 0.9 copy-start.1
  25.2 0.9 copy-start.3
  68.2 6.6 %copy-start = (f32[4,2,128,128]{3,2,1,0:T(8,128)S(1)}, f32[4,2,128,128]{3,2,1,0:T(8,128)}, u32[]{:S(2)}) copy-start(f32[4,2,128,128]{3,2,1,0:T(8,128)} %param.24) | copy-start | bytes 1572868
  69.0 22.0 %collective-permute-start.4 = (f32[2,128,384]{2,1,0:T(8,128)}, f32[2,128,384]{2,1,0:T(8,128)S(1)}, u32[]{:S(2)}, u32[]{:S(2)}) collective-permute-start(f32[2,128,384]{2,1,0:T(8,128)} %get-tuple-element.457), channel_id=1, source_target_pairs={{0,2},{2,4},{4,6},{6,8},{8,10},{10,12},{12,14},{1,3},{3,5},{5,7},{... | collective-permute-start | bytes 1179656 | tf_op jit(solution)/shard_map/ppermute | solution.py:17
  73.5 17.5 %collective-permute-start.5 = (f32[2,128,384]{2,1,0:T(8,128)S(1)}, f32[2,128,384]{2,1,0:T(8,128)S(1)}, u32[]{:S(2)}, u32[]{:S(2)}) collective-permute-start(f32[2,128,384]{2,1,0:T(8,128)S(1)} %get-tuple-element.458), channel_id=1, source_target_pairs={{2,0},{4,2},{6,4},{8,6},{10,8},{12,10},{14,12},{3,1},{5,3},{7,5},{... | collective-permute-start | bytes 1179656 | tf_op jit(solution)/shard_map/ppermute | solution.py:20
  91.1 81.0 %copy-start.2 = (f32[2,128,128]{2,1,0:T(8,128)S(1)}, f32[2,128,128]{2,1,0:T(8,128)}, u32[]{:S(2)}) copy-start(f32[2,128,128]{2,1,0:T(8,128)} %param.23) | copy-start | bytes 393220
  91.1 81.0 %collective-permute-start.6 = (f32[2,128,128]{2,1,0:T(8,128)S(1)}, f32[2,128,128]{2,1,0:T(8,128)S(1)}, u32[]{:S(2)}, u32[]{:S(2)}) collective-permute-start(f32[2,128,128]{2,1,0:T(8,128)S(1)} %get-tuple-element.459), channel_id=1, source_target_pairs={{0,1},{2,3},{4,5},{6,7},{8,9},{10,11},{12,13},{14,15},{16,17},{18,... | collective-permute-start | bytes 393224 | tf_op jit(solution)/shard_map/ppermute | solution.py:17
  92.6 79.5 %collective-permute-start.7 = (f32[2,128,128]{2,1,0:T(8,128)S(1)}, f32[2,128,128]{2,1,0:T(8,128)S(1)}, u32[]{:S(2)}, u32[]{:S(2)}) collective-permute-start(f32[2,128,128]{2,1,0:T(8,128)S(1)} %get-tuple-element.460), channel_id=1, source_target_pairs={{1,0},{3,2},{5,4},{7,6},{9,8},{11,10},{13,12},{15,14},{17,16},{19,... | collective-permute-start | bytes 393224 | tf_op jit(solution)/shard_map/ppermute | solution.py:20
Sparse Core Ops, SparseCore 0:
  77.1 93.0 all-reduce.1
where the time goes:
time: 180 us
  waiting for transfers between devices  96.5 us (54%)
  matrix products  23.8 us (13%)
  starting transfers between devices  17.3 us (10%)
  between operations  14.8 us (8%)
  local copies, waits for them, and re-layouts  12.6 us (7%)
  loops' own time  9.63 us (5%)
  other arithmetic  4.97 us (3%)
    psum x1, waiting for transfers between devices, body(): summed = lax.psum(probe_grad, ('row', 'col'))  76.3 us
    ppermute x4, waiting for transfers between devices, with_halo(): lax.ppermute(lax.slice_in_dim(block, block.shape[dim] - width, None, axis...  15.8 us
    ppermute x4, starting transfers between devices, with_halo(): lax.ppermute(lax.slice_in_dim(block, block.shape[dim] - width, None, axis...  12.1 us
    another operation x1, loops' own time, body(): gradient, probe_grad = lax.fori_loop(0, slot_total, slot_step, start_carry)  9.63 us
    ppermute x4, starting transfers between devices, with_halo(): lax.ppermute(lax.slice_in_dim(block, 0, width, axis=dim), axis, backward)  5.17 us
    dynamic_update_slice x2, local copies, waits for them, and re-layouts, slot_step(): lax.dynamic_update_slice(local_grad, region, (as_index(0), corner_y, corn...  4.66 us
    ppermute x4, waiting for transfers between devices, with_halo(): lax.ppermute(lax.slice_in_dim(block, 0, width, axis=dim), axis, backward)  4.31 us
  transfers between devices with their start and end apart: 9, of which 5 were waited for; matrix products, arithmetic and copies ran while one was open for 3% of the time, Pallas kernels for 0%

commit v1 on v0

--- a/solution.py
+++ b/solution.py
@@ -7,6 +7,10 @@
 object_rate = 1.0
 probe_rate = 1.0
 epsilon = 1e-06
+
+
+def things_run(inp, along_axis):
+    return jnp.sum(lax.all_gather(inp, axis_name=along_axis), 0)
 
 
 def with_halo(block, sides, width):
@@ -125,7 +129,7 @@
         jnp.max(jnp.sum(probe[:, 0] * probe[:, 0] + probe[:, 1] * probe[:, 1], axis=0)) + epsilon
     )
     object_field = object_field - object_rate * object_grad / weight
-    summed = lax.psum(probe_grad, ("row", "col"))
+    summed = things_run(probe_grad, ("row", "col"))
     probe = probe - probe_rate * summed / tile_total
     return (object_field, probe)
 

time: 180 us -> 165 us (0.917)
  waiting for transfers between devices: 96.5 us -> 80 us
  other arithmetic: 4.97 us -> 7.09 us
    psum x1 -> x0, waiting for transfers between devices: 76.3 us -> none  [body(): summed = lax.psum(probe_grad, ('row', 'col'))]
    all_gather x0 -> x1, waiting for transfers between devices: none -> 52.9 us  [things_run(): return jnp.sum(lax.all_gather(inp, axis_name=along_axis), 0)]
    ppermute x4, waiting for transfers between devices: 15.8 us -> 22.2 us  [with_halo(): lax.ppermute(lax.slice_in_dim(block, block.shape[dim] - width, None, axis...]
    reduce_sum x0 -> x1, other arithmetic: none -> 3.94 us  [things_run(): return jnp.sum(lax.all_gather(inp, axis_name=along_axis), 0)]
    sub x1, other arithmetic: 1.89 us -> 0.06 us  [body(): probe = probe - probe_rate * summed / tile_total]
    unnamed x11 -> x14, local copies, waits for them, and re-layouts: 2.84 us -> 4.46 us
  transfers between devices with their start and end apart: 9 -> 9, of which waited for: 5 -> 6; matrix products, arithmetic and copies ran while one was open for 3% -> 2% of each run, Pallas kernels for 0% -> 0%
where the time goes in v1:
time: 165 us
  waiting for transfers between devices  80 us (48%)
  matrix products  23.8 us (14%)
  starting transfers between devices  17.5 us (11%)
  between operations  14.9 us (9%)
  local copies, waits for them, and re-layouts  12.6 us (8%)
  loops' own time  8.91 us (5%)
  other arithmetic  7.09 us (4%)
    all_gather x1, waiting for transfers between devices, things_run(): return jnp.sum(lax.all_gather(inp, axis_name=along_axis), 0)  52.9 us
    ppermute x4, waiting for transfers between devices, with_halo(): lax.ppermute(lax.slice_in_dim(block, block.shape[dim] - width, None, axis...  22.2 us
    ppermute x4, starting transfers between devices, with_halo(): lax.ppermute(lax.slice_in_dim(block, block.shape[dim] - width, None, axis...  12.1 us
    another operation x1, loops' own time, body(): gradient, probe_grad = lax.fori_loop(0, slot_total, slot_step, start_carry)  8.91 us
    ppermute x4, starting transfers between devices, with_halo(): lax.ppermute(lax.slice_in_dim(block, 0, width, axis=dim), axis, backward)  5.3 us
    ppermute x4, waiting for transfers between devices, with_halo(): lax.ppermute(lax.slice_in_dim(block, 0, width, axis=dim), axis, backward)  4.92 us
    dynamic_update_slice x2, local copies, waits for them, and re-layouts, slot_step(): lax.dynamic_update_slice(local_grad, region, (as_index(0), corner_y, corn...  4.66 us
    unnamed x14, local copies, waits for them, and re-layouts  4.46 us
  transfers between devices with their start and end apart: 9, of which 6 were waited for; matrix products, arithmetic and copies ran while one was open for 2% of the time, Pallas kernels for 0%

profile of v1, /device:TPU:0, one launch (start us, length us, event | category | flops | bytes accessed | tf_op | source)
XLA Modules:
  0.0 164.8 jit_solution(12804561972044171489)
XLA Ops:
  7.2 4.9 %collective-permute-start = (f32[2,128,128]{2,1,0:T(8,128)}, f32[2,128,128]{2,1,0:T(8,128)S(1)}, u32[]{:S(2)}, u32[]{:S(2)}) collective-permute-start(f32[2,128,128]{2,1,0:T(8,128)} %param.23), channel_id=1, source_target_pairs={{0,2},{2,4},{4,6},{6,8},{8,10},{10,12},{12,14},{1,3},{3,5},{5,7},{... | collective-permute-start | bytes 393224 | tf_op jit(solution)/shard_map/ppermute | solution.py:21
  12.1 1.3 collective-permute-start.1
  13.4 1.7 %collective-permute-done = f32[2,128,128]{2,1,0:T(8,128)S(1)} collective-permute-done((f32[2,128,128]{2,1,0:T(8,128)}, f32[2,128,128]{2,1,0:T(8,128)S(1)}, u32[]{:S(2)}, u32[]{:S(2)}) %collective-permute-start) | collective-permute-done | bytes 131104 | tf_op jit(solution)/shard_map/ppermute | solution.py:21
  15.2 0.9 constant_dynamic-update-slice_fusion.1
  16.1 3.1 %collective-permute-done.1 = f32[2,128,128]{2,1,0:T(8,128)S(1)} collective-permute-done((f32[2,128,128]{2,1,0:T(8,128)}, f32[2,128,128]{2,1,0:T(8,128)S(1)}, u32[]{:S(2)}, u32[]{:S(2)}) %collective-permute-start.1) | collective-permute-done | bytes 131104 | tf_op jit(solution)/shard_map/ppermute | solution.py:24
  19.2 1.3 collective-permute-start.2
  20.5 1.3 collective-permute-start.3
  21.8 1.1 copy.59
  22.9 1.2 collective-permute-done.3
  24.1 1.1 pad_maximum_fusion
  25.3 0.8 copy-done.2
  26.1 41.3 %while.26 = (s32[]{:T(128)}, f32[2,384,384]{2,1,0:T(8,128)S(1)}, f32[4,2,128,128]{3,2,0,1:T(8,128)S(1)}, s32[1,1,2,2]{3,2,1,0:T(2,128)S(1)}, s32[]{:T(128)}, /*i...) while((s32[]{:T(128)}, f32[2,384,384]{2,1,0:T(8,128)S(1)}, ...), condition=%wide.region_4.5_spmd.clone.clone, body=%wide.region_0.4_spmd.clone.clone.sunk | while | flops 1617952768 | bytes 16646421 | solution.py:111
  30.4 1.1 dynamic-slice_bitcast_fusion.3
  44.4 2.2 %dynamic_update_slice.11 = f32[2,384,384]{2,1,0:T(8,128)S(1)} dynamic-update-slice(f32[2,384,384]{2,1,0:T(8,128)S(1)} %get-tuple-element.555, f32[2,128,128]{2,1,0:T(8,128)S(1)} %fusion.247, s32[]{:T(128)} %constant.191.clone.1..sunk, s32[]{:T(128)S(6)} %select_n.177, s32[]{:T(128)S(6)} %select_n.178) | dynamic-update-slice | bytes 262148 | tf_op jit(solution)/shard_map/while/body/eval_jaxpr/dynamic_update_slice | solution.py:107
  50.8 1.1 dynamic-slice_bitcast_fusion.3
  64.9 2.5 %dynamic_update_slice.11 = f32[2,384,384]{2,1,0:T(8,128)S(1)} dynamic-update-slice(f32[2,384,384]{2,1,0:T(8,128)S(1)} %get-tuple-element.555, f32[2,128,128]{2,1,0:T(8,128)S(1)} %fusion.247, s32[]{:T(128)} %constant.191.clone.1..sunk, s32[]{:T(128)S(6)} %select_n.177, s32[]{:T(128)S(6)} %select_n.178) | dynamic-update-slice | bytes 262148 | tf_op jit(solution)/shard_map/while/body/eval_jaxpr/dynamic_update_slice | solution.py:107
  68.3 4.6 %collective-permute-start.4 = (f32[2,128,384]{2,1,0:T(8,128)S(1)}, f32[2,128,384]{2,1,0:T(8,128)S(1)}, u32[]{:S(2)}, u32[]{:S(2)}) collective-permute-start(f32[2,128,384]{2,1,0:T(8,128)S(1)} %get-tuple-element.469), channel_id=1, source_target_pairs={{0,2},{2,4},{4,6},{6,8},{8,10},{10,12},{12,14},{1,3},{3,5},{5,7},{... | collective-permute-start | bytes 1179656 | tf_op jit(solution)/shard_map/ppermute | solution.py:21
  73.0 1.4 collective-permute-start.5
  74.4 20.5 %collective-permute-done.4 = f32[2,128,384]{2,1,0:T(8,128)S(1)} collective-permute-done((f32[2,128,384]{2,1,0:T(8,128)S(1)}, f32[2,128,384]{2,1,0:T(8,128)S(1)}, u32[]{:S(2)}, u32[]{:S(2)}) %collective-permute-start.4) | collective-permute-done | bytes 393248 | tf_op jit(solution)/shard_map/ppermute | solution.py:21
  95.0 1.3 collective-permute-start.6
  96.3 1.3 collective-permute-start.7
  100.2 52.9 %all-gather.3.cloned.1.call-done = f32[64,2,128,128]{3,2,0,1:T(8,128)} async-done(((f32[4,2,128,128]{3,2,0,1:T(8,128)}), f32[64,2,128,128]{3,2,0,1:T(8,128)}) %all-gather.3.cloned.1.call-update) | async-done | bytes 8388624 | tf_op jit(solution)/shard_map/all_gather | solution.py:13
  153.1 3.9 %reduce_sum.61 = f32[4,2,128,128]{3,2,0,1:T(8,128)S(1)} reduce(f32[16,4,2,128,128]{4,3,1,0,2:T(8,128)} %bitcast.195, f32[]{:T(128)} %constant.192.clone.1), dimensions={0}, to_apply=%region_7.8 | reduce | flops 1966080 | bytes 8912900 | tf_op jit(solution)/shard_map/reduce_sum | solution.py:13
  157.1 0.8 copy.61
  (66 shorter events, 28.7 us)
Async XLA Ops:
  7.2 145.9 %all-gather.3.cloned.1.call-start = ((), (), s32[]{:S(2)}) async-start(), calls=%async_computation | async-start | bytes 8912896 | tf_op jit(solution)/shard_map/all_gather | solution.py:13
  7.2 7.9 %collective-permute-start = (f32[2,128,128]{2,1,0:T(8,128)}, f32[2,128,128]{2,1,0:T(8,128)S(1)}, u32[]{:S(2)}, u32[]{:S(2)}) collective-permute-start(f32[2,128,128]{2,1,0:T(8,128)} %param.23), channel_id=1, source_target_pairs={{0,2},{2,4},{4,6},{6,8},{8,10},{10,12},{12,14},{1,3},{3,5},{5,7},{... | collective-permute-start | bytes 393224 | tf_op jit(solution)/shard_map/ppermute | solution.py:21
  12.1 7.1 %collective-permute-start.1 = (f32[2,128,128]{2,1,0:T(8,128)}, f32[2,128,128]{2,1,0:T(8,128)S(1)}, u32[]{:S(2)}, u32[]{:S(2)}) collective-permute-start(f32[2,128,128]{2,1,0:T(8,128)} %param.23), channel_id=1, source_target_pairs={{2,0},{4,2},{6,4},{8,6},{10,8},{12,10},{14,12},{3,1},{5,3},{7,5},{... | collective-permute-start | bytes 393224 | tf_op jit(solution)/shard_map/ppermute | solution.py:24
  19.2 3.7 %collective-permute-start.2 = (f32[2,384,128]{2,1,0:T(8,128)S(1)}, f32[2,384,128]{2,1,0:T(8,128)S(1)}, u32[]{:S(2)}, u32[]{:S(2)}) collective-permute-start(f32[2,384,128]{2,1,0:T(8,128)S(1)} %constant_dynamic-update-slice_fusion), channel_id=1, source_target_pairs={{0,1},{2,3},{4,5},{6,7},{8,9},{10,11},{12,13},{14,15},{16,17},{18,... | collective-permute-start | bytes 1179656 | tf_op jit(solution)/shard_map/ppermute | solution.py:21
  20.5 3.6 %collective-permute-start.3 = (f32[2,384,128]{2,1,0:T(8,128)S(1)}, f32[2,384,128]{2,1,0:T(8,128)S(1)}, u32[]{:S(2)}, u32[]{:S(2)}) collective-permute-start(f32[2,384,128]{2,1,0:T(8,128)S(1)} %constant_dynamic-update-slice_fusion), channel_id=1, source_target_pairs={{1,0},{3,2},{5,4},{7,6},{9,8},{11,10},{13,12},{15,14},{17,16},{19,... | collective-permute-start | bytes 1179656 | tf_op jit(solution)/shard_map/ppermute | solution.py:24
  25.2 0.9 copy-start.2
  25.2 0.9 copy-start.4
  67.4 0.8 copy-start
  68.3 29.3 %copy-start.1 = (f32[4,2,128,128]{3,2,1,0:T(8,128)S(1)}, f32[4,2,128,128]{3,2,1,0:T(8,128)}, u32[]{:S(2)}) copy-start(f32[4,2,128,128]{3,2,1,0:T(8,128)} %param.24) | copy-start | bytes 1572868
  68.3 26.6 %collective-permute-start.4 = (f32[2,128,384]{2,1,0:T(8,128)S(1)}, f32[2,128,384]{2,1,0:T(8,128)S(1)}, u32[]{:S(2)}, u32[]{:S(2)}) collective-permute-start(f32[2,128,384]{2,1,0:T(8,128)S(1)} %get-tuple-element.469), channel_id=1, source_target_pairs={{0,2},{2,4},{4,6},{6,8},{8,10},{10,12},{12,14},{1,3},{3,5},{5,7},{... | collective-permute-start | bytes 1179656 | tf_op jit(solution)/shard_map/ppermute | solution.py:21
  73.0 26.6 %copy-start.3 = (f32[2,128,128]{2,1,0:T(8,128)S(1)}, f32[2,128,128]{2,1,0:T(8,128)}, u32[]{:S(2)}) copy-start(f32[2,128,128]{2,1,0:T(8,128)} %param.23) | copy-start | bytes 393220
  73.0 21.9 %collective-permute-start.5 = (f32[2,128,384]{2,1,0:T(8,128)S(1)}, f32[2,128,384]{2,1,0:T(8,128)S(1)}, u32[]{:S(2)}, u32[]{:S(2)}) collective-permute-start(f32[2,128,384]{2,1,0:T(8,128)S(1)} %get-tuple-element.470), channel_id=1, source_target_pairs={{2,0},{4,2},{6,4},{8,6},{10,8},{12,10},{14,12},{3,1},{5,3},{7,5},{... | collective-permute-start | bytes 1179656 | tf_op jit(solution)/shard_map/ppermute | solution.py:24
  95.0 3.9 %collective-permute-start.6 = (f32[2,128,128]{2,1,0:T(8,128)S(1)}, f32[2,128,128]{2,1,0:T(8,128)S(1)}, u32[]{:S(2)}, u32[]{:S(2)}) collective-permute-start(f32[2,128,128]{2,1,0:T(8,128)S(1)} %get-tuple-element.471), channel_id=1, source_target_pairs={{0,1},{2,3},{4,5},{6,7},{8,9},{10,11},{12,13},{14,15},{16,17},{18,... | collective-permute-start | bytes 393224 | tf_op jit(solution)/shard_map/ppermute | solution.py:21
  96.3 3.2 %collective-permute-start.7 = (f32[2,128,128]{2,1,0:T(8,128)S(1)}, f32[2,128,128]{2,1,0:T(8,128)S(1)}, u32[]{:S(2)}, u32[]{:S(2)}) collective-permute-start(f32[2,128,128]{2,1,0:T(8,128)S(1)} %get-tuple-element.472), channel_id=1, source_target_pairs={{1,0},{3,2},{5,4},{7,6},{9,8},{11,10},{13,12},{15,14},{17,16},{19,... | collective-permute-start | bytes 393224 | tf_op jit(solution)/shard_map/ppermute | solution.py:24
Sparse Core Ops, SparseCore 0:
  68.4 84.6 all-gather.2
